TPU v7x, 8 devices: a whole 2x2x1 slice. The times are simulated.
8 devices in a mesh: dp: 1 (over z), sp: 8 (over y, x, core).
Axes of the slice: x: 2, y: 2, z: 1, core: 2. Of those that a mesh axis runs over, the one named last changes fastest.
Arguments:
- hidden: bfloat16 [8, 2048, 2048], P('dp', 'sp')
- d_out: bfloat16 [8, 2048, 2048], P('dp', 'sp')
- positions: int32 [8, 2048], P('dp', 'sp')
- norm_gain: bfloat16 [2048], replicated
- w_query: bfloat16 [2048, 2048], replicated
- b_query: bfloat16 [2048], replicated
- w_key: bfloat16 [2048, 256], replicated
- b_key: bfloat16 [256], replicated
- w_value: bfloat16 [2048, 256], replicated
- b_value: bfloat16 [256], replicated
- w_out: bfloat16 [2048, 2048], replicated
Outputs:
- output 1: bfloat16 [8, 2048, 2048], P('dp', 'sp')
- output 2: bfloat16 [8, 2048, 2048], P('dp', 'sp')
- output 3: float32 [2048], P('dp')
- output 4: float32 [2048, 2048], P('dp')
- output 5: float32 [2048], P('dp')
- output 6: float32 [2048, 256], P('dp')
- output 7: float32 [256], P('dp')
- output 8: float32 [2048, 256], P('dp')
- output 9: float32 [256], P('dp')
- output 10: float32 [2048, 2048], P('dp')
All inputs are finite; a program needn't handle non-finite values.
Results may differ from a plain program's by a relative error of at most 0.02.
Values are sent between devices in bfloat16 or wider.
A program may use at most 1 GiB of HBM per device.

v0:
```python
import math
import jax
import jax.numpy as jnp
from jax import lax
from jax.sharding import PartitionSpec as P

HEAD_DIM = 128
ROPE_BASE = 1000000.0
NORM_EPS = 1e-6


def rope_tables(positions):
    half_dim = HEAD_DIM // 2
    inv_freq = ROPE_BASE ** (-jnp.arange(half_dim, dtype=jnp.float32) * (2.0 / HEAD_DIM))
    angles = positions.astype(jnp.float32)[..., None] * inv_freq
    return jnp.cos(angles)[:, :, None, :], jnp.sin(angles)[:, :, None, :]


def rotate(vec, cosine, sine):
    half_dim = vec.shape[-1] // 2
    first = vec[..., :half_dim]
    second = vec[..., half_dim:]
    return jnp.concatenate([first * cosine - second * sine, second * cosine + first * sine], axis=-1)


def norm_forward(hidden, norm_gain):
    hidden_f = hidden.astype(jnp.float32)
    inv_rms = lax.rsqrt(jnp.mean(hidden_f * hidden_f, axis=-1, keepdims=True) + NORM_EPS)
    unit = hidden_f * inv_rms
    return (unit * norm_gain.astype(jnp.float32)).astype(jnp.bfloat16), unit, inv_rms


def norm_backward(d_normed, unit, inv_rms, norm_gain):
    d_unit = d_normed * norm_gain.astype(jnp.float32)
    d_input = inv_rms * (d_unit - unit * jnp.mean(d_unit * unit, axis=-1, keepdims=True))
    return d_input, d_normed * unit


def block_size(batch, heads, seq):
    return math.gcd(seq, max(8, (1 << 24) // (batch * heads * seq)))


def attn_forward(query, keys, values):
    batch, seq, kv_local, group, head_dim = query.shape
    block_len = block_size(batch, kv_local * group, seq)
    n_blocks = seq // block_len
    scale = head_dim ** -0.5
    key_pos = jnp.arange(seq)

    def one_block(index):
        q_block = lax.dynamic_slice_in_dim(query, index * block_len, block_len, axis=1)
        scores = jnp.einsum('bqkgd,bskd->bkgqs', q_block, keys, preferred_element_type=jnp.float32) * scale
        q_pos = index * block_len + jnp.arange(block_len)
        scores = jnp.where(key_pos[None, :] <= q_pos[:, None], scores, -1e30)
        peak = jnp.max(scores, axis=-1, keepdims=True)
        exp_scores = jnp.exp(scores - peak)
        total = jnp.sum(exp_scores, axis=-1, keepdims=True)
        probs = (exp_scores / total).astype(jnp.bfloat16)
        out_block = jnp.einsum('bkgqs,bskd->bqkgd', probs, values, preferred_element_type=jnp.float32)
        return out_block.astype(jnp.bfloat16), (peak + jnp.log(total))[..., 0]

    out_blocks, lse_blocks = lax.map(one_block, jnp.arange(n_blocks))
    attended = jnp.moveaxis(out_blocks, 0, 1).reshape(batch, seq, kv_local, group, head_dim)
    return attended, lse_blocks


def attn_backward(query, keys, values, lse_blocks, d_att, delta):
    batch, seq, kv_local, group, head_dim = query.shape
    block_len = block_size(batch, kv_local * group, seq)
    n_blocks = seq // block_len
    scale = head_dim ** -0.5
    key_pos = jnp.arange(seq)

    def one_block(carry, index):
        d_keys, d_values = carry
        start = index * block_len
        q_block = lax.dynamic_slice_in_dim(query, start, block_len, axis=1)
        do_block = lax.dynamic_slice_in_dim(d_att, start, block_len, axis=1)
        delta_block = lax.dynamic_slice_in_dim(delta, start, block_len, axis=3)
        lse_block = lax.dynamic_index_in_dim(lse_blocks, index, axis=0, keepdims=False)
        scores = jnp.einsum('bqkgd,bskd->bkgqs', q_block, keys, preferred_element_type=jnp.float32) * scale
        q_pos = start + jnp.arange(block_len)
        scores = jnp.where(key_pos[None, :] <= q_pos[:, None], scores, -1e30)
        probs = jnp.exp(scores - lse_block[..., None])
        d_probs = jnp.einsum('bqkgd,bskd->bkgqs', do_block, values, preferred_element_type=jnp.float32)
        d_scores = (probs * (d_probs - delta_block[..., None]) * scale).astype(jnp.bfloat16)
        d_values = d_values + jnp.einsum('bkgqs,bqkgd->bskd', probs.astype(jnp.bfloat16), do_block,
                                         preferred_element_type=jnp.float32)
        d_keys = d_keys + jnp.einsum('bkgqs,bqkgd->bskd', d_scores, q_block, preferred_element_type=jnp.float32)
        dq_block = jnp.einsum('bkgqs,bskd->bqkgd', d_scores, keys, preferred_element_type=jnp.float32)
        return (d_keys, d_values), dq_block.astype(jnp.bfloat16)

    zeros = jnp.zeros(keys.shape, jnp.float32)
    (d_keys, d_values), dq_blocks = lax.scan(one_block, (zeros, zeros), jnp.arange(n_blocks))
    d_query = jnp.moveaxis(dq_blocks, 0, 1).reshape(query.shape)
    return d_query, d_keys, d_values


def solution(mesh):
    sp_size = mesh.shape['sp']

    def device_step(hidden, d_out, positions, norm_gain, w_query, b_query, w_key, b_key, w_value, b_value, w_out):
        batch, tokens, d_model = hidden.shape
        seq = tokens * sp_size
        q_heads = d_model // HEAD_DIM
        kv_heads = w_key.shape[1] // HEAD_DIM
        kv_width = kv_heads * HEAD_DIM
        kv_dup = max(kv_heads, sp_size)
        copies = kv_dup // kv_heads
        heads_local = q_heads // sp_size
        kv_local = kv_dup // sp_size
        group = heads_local // kv_local
        cosine, sine = rope_tables(positions)

        normed, unit, inv_rms = norm_forward(hidden, norm_gain)
        q_pre = jnp.einsum('btd,de->bte', normed, w_query, preferred_element_type=jnp.float32) + b_query.astype(jnp.float32)
        query = rotate(q_pre.reshape(batch, tokens, q_heads, HEAD_DIM), cosine, sine).astype(jnp.bfloat16)
        k_pre = jnp.einsum('btd,de->bte', normed, w_key, preferred_element_type=jnp.float32) + b_key.astype(jnp.float32)
        keys = rotate(k_pre.reshape(batch, tokens, kv_heads, HEAD_DIM), cosine, sine).astype(jnp.bfloat16)
        v_pre = jnp.einsum('btd,de->bte', normed, w_value, preferred_element_type=jnp.float32) + b_value.astype(jnp.float32)
        values = v_pre.astype(jnp.bfloat16).reshape(batch, tokens, kv_heads, HEAD_DIM)
        if copies > 1:
            keys = jnp.repeat(keys, copies, axis=2)
            values = jnp.repeat(values, copies, axis=2)

        query_h = lax.all_to_all(query, 'sp', 2, 1, tiled=True).reshape(batch, seq, kv_local, group, HEAD_DIM)
        keys_h = lax.all_to_all(keys, 'sp', 2, 1, tiled=True)
        values_h = lax.all_to_all(values, 'sp', 2, 1, tiled=True)
        attended_h, lse_blocks = attn_forward(query_h, keys_h, values_h)
        attended = lax.all_to_all(attended_h.reshape(batch, seq, heads_local, HEAD_DIM), 'sp', 1, 2, tiled=True)
        attended = attended.reshape(batch, tokens, d_model)
        proj = jnp.einsum('btd,de->bte', attended, w_out, preferred_element_type=jnp.float32)
        block_out = (hidden.astype(jnp.float32) + proj).astype(jnp.bfloat16)

        d_w_out = jnp.einsum('btd,bte->de', attended, d_out, preferred_element_type=jnp.float32)
        d_att = jnp.einsum('bte,de->btd', d_out, w_out, preferred_element_type=jnp.float32).astype(jnp.bfloat16)
        d_att_h = lax.all_to_all(d_att.reshape(batch, tokens, q_heads, HEAD_DIM), 'sp', 2, 1, tiled=True)
        d_att_h = d_att_h.reshape(batch, seq, kv_local, group, HEAD_DIM)
        delta = jnp.einsum('bskgd,bskgd->bkgs', d_att_h, attended_h, preferred_element_type=jnp.float32)
        dq_h, dk_h, dv_h = attn_backward(query_h, keys_h, values_h, lse_blocks, d_att_h, delta)

        d_query = lax.all_to_all(dq_h.reshape(batch, seq, heads_local, HEAD_DIM), 'sp', 1, 2, tiled=True)
        wire_type = jnp.float32 if copies > 1 else jnp.bfloat16
        d_keys = lax.all_to_all(dk_h.astype(wire_type), 'sp', 1, 2, tiled=True)
        d_values = lax.all_to_all(dv_h.astype(wire_type), 'sp', 1, 2, tiled=True)
        if copies > 1:
            d_keys = jnp.sum(d_keys.reshape(batch, tokens, kv_heads, copies, HEAD_DIM), axis=3)
            d_values = jnp.sum(d_values.reshape(batch, tokens, kv_heads, copies, HEAD_DIM), axis=3)

        dq_pre = rotate(d_query.astype(jnp.float32), cosine, -sine).reshape(batch, tokens, d_model)
        dk_pre = rotate(d_keys.astype(jnp.float32), cosine, -sine).reshape(batch, tokens, kv_width)
        dv_pre = d_values.astype(jnp.float32).reshape(batch, tokens, kv_width)
        dq_bf = dq_pre.astype(jnp.bfloat16)
        dk_bf = dk_pre.astype(jnp.bfloat16)
        dv_bf = dv_pre.astype(jnp.bfloat16)
        d_w_query = jnp.einsum('btd,bte->de', normed, dq_bf, preferred_element_type=jnp.float32)
        d_w_key = jnp.einsum('btd,bte->de', normed, dk_bf, preferred_element_type=jnp.float32)
        d_w_value = jnp.einsum('btd,bte->de', normed, dv_bf, preferred_element_type=jnp.float32)
        d_normed = (jnp.einsum('bte,de->btd', dq_bf, w_query, preferred_element_type=jnp.float32)
                    + jnp.einsum('bte,de->btd', dk_bf, w_key, preferred_element_type=jnp.float32)
                    + jnp.einsum('bte,de->btd', dv_bf, w_value, preferred_element_type=jnp.float32))
        d_input, gain_terms = norm_backward(d_normed, unit, inv_rms, norm_gain)
        d_hidden = (d_out.astype(jnp.float32) + d_input).astype(jnp.bfloat16)
        grads = lax.psum((jnp.sum(gain_terms, axis=(0, 1)), d_w_query, jnp.sum(dq_pre, axis=(0, 1)),
                          d_w_key, jnp.sum(dk_pre, axis=(0, 1)), d_w_value, jnp.sum(dv_pre, axis=(0, 1)),
                          d_w_out), 'sp')
        return (block_out, d_hidden) + tuple(grads)

    seq_spec = P('dp', 'sp', None)
    in_specs = (seq_spec, seq_spec, P('dp', 'sp'), P(), P(), P(), P(), P(), P(), P(), P())
    out_specs = (seq_spec, seq_spec, P('dp'), P('dp', None), P('dp'), P('dp', None), P('dp'),
                 P('dp', None), P('dp'), P('dp', None))
    return jax.shard_map(device_step, mesh=mesh, in_specs=in_specs, out_specs=out_specs, check_vma=False)
```

profile of v0, /device:TPU:0, one launch (start us, length us, event | category | flops | bytes accessed | tf_op | source)
XLA Modules:
  0.0 2254.7 jit_solution(16071787915748369872)
XLA Ops:
  45.5 40.3 %all-to-all-done.1 = bf16[8,256,8,128]{3,1,0,2:T(8,128)(2,1)} async-done(((bf16[8,256,8,128]{3,1,0,2:T(8,128)(2,1)}), bf16[8,256,8,128]{3,1,0,2:T(8,128)(2,1)}, u32[]{:S(2)}, u32[]{:S(2)}) %all-to-all-start.1) | async-done | bytes 4194336 | tf_op jit(solution)/shard_map/all_to_all | solution.py:127
  92.2 23.7 %convert_bitcast_fusion.2 = bf16[8,32,16,8,128]{4,3,2,1,0:T(8,128)(2,1)} fusion(bf16[8,256,2048]{2,1,0:T(8,128)(2,1)} %param.16, bf16[2048,2048]{1,0:T(8,128)(2,1)} %param.25), kind=kOutput, calls=%fused_computation.99 | convolution fusion | flops 17184063488 | bytes 25165824 | tf_op jit(solution)/shard_map/bte,de->btd/dot_general | solution.py:136
  145.1 24.4 %broadcast_add_fusion = f32[8,256,2048]{2,1,0:T(8,128)} fusion(f32[2048]{0:T(1024)S(1)} %convert_element_type.106, bf16[2048,2048]{1,0:T(8,128)(2,1)} %param.19, bf16[8,256,2048]{2,1,0:T(8,128)(2,1)} %param.15, f32[2048]{0:T(1024)S(1)} %convert_element_type.104, f32[8,256]{1,0:T(8,128)S(1)} %add_rsqrt_fusion), kind=kOutput, calls=%fused_computation.100 | convolution fusion | flops 17200840704 | bytes 33579008 | tf_op jit(solution)/shard_map/btd,de->bte/dot_general | solution.py:116
  192.9 21.4 subtract_convert_fusion
  260.1 76.7 %all-to-all-done = bf16[8,256,16,128]{3,1,0,2:T(8,128)(2,1)} async-done(((bf16[8,256,16,128]{3,1,0,2:T(8,128)(2,1)}), bf16[8,256,16,128]{3,1,0,2:T(8,128)(2,1)}, u32[]{:S(2)}, u32[]{:S(2)}) %all-to-all-start) | async-done | bytes 8388640 | tf_op jit(solution)/shard_map/all_to_all | solution.py:126
  350.1 317.2 %while.28 = (s32[]{:T(128)}, bf16[4,8,512,1,2,128]{5,2,0,4,1,3:T(8,128)(2,1)}, f32[4,8,1,2,512]{4,3,1,2,0:T(2,128)S(1)}, s32[4]{0:T(128)S(1)}, bf16[8,2048,1,2,1...) while((s32[]{:T(128)}, ...), condition=%wide.region_4.5_spmd.clone, body=%wide.region_1.4_spmd.clone.sunk | while | flops 8793350144 | bytes 218370224 | solution.py:62
  352.5 26.1 %fusion.140 = (f32[8,2,512]{2,1,0:T(2,128)S(1)}, f32[8,512,2,2048]{3,1,2,0:T(8,128)}) fusion(pred[512,2048]{1,0:T(8,128)(4,1)S(1)} %iota_compare_fusion.4, bf16[8,2048,1,128]{3,1,0,2:T(8,128)(2,1)} %get-tuple-element.383, bf16[8,2048,1,2,128]{4,1,3,0,2:T(8,128)(2,1)} %get-tuple-element.382, s32[]{:T(128)S(6)} %select_n.64), kind=kOutput, calls=%fused_computation.6.clone.1 | convolution fusion | flops 4345290752 | bytes 74481664 | tf_op jit(solution)/shard_map/while/body/eval_jaxpr/bqkgd,bskd->bkgqs/dot_general | solution.py:52
  378.6 21.5 fusion.141
  400.1 29.6 %bitcast_dynamic-update-slice_fusion.6 = bf16[4,8,512,1,2,128]{5,2,0,4,1,3:T(8,128)(2,1)} fusion(bf16[4,8,512,1,2,128]{5,2,0,4,1,3:T(8,128)(2,1)} %get-tuple-element.368, s32[]{:T(128)S(6)} %copy.394, bf16[8,2048,1,128]{3,1,0,2:T(8,128)(2,1)} %get-tuple-element.384, f32[8,2,512]{2,1,0:T(2,128)S(1)} %fusion.141, ...), kind=kOutput, calls=%fused_computation.13.clone.1 | convolution fusion | flops 4379901952 | bytes 74514432 | tf_op jit(solution)/shard_map/while/body/eval_jaxpr/bkgqs,bskd->bqkgd/dot_general | solution.py:59
  431.7 26.1 %fusion.140 = (f32[8,2,512]{2,1,0:T(2,128)S(1)}, f32[8,512,2,2048]{3,1,2,0:T(8,128)}) fusion(pred[512,2048]{1,0:T(8,128)(4,1)S(1)} %iota_compare_fusion.4, bf16[8,2048,1,128]{3,1,0,2:T(8,128)(2,1)} %get-tuple-element.383, bf16[8,2048,1,2,128]{4,1,3,0,2:T(8,128)(2,1)} %get-tuple-element.382, s32[]{:T(128)S(6)} %select_n.64), kind=kOutput, calls=%fused_computation.6.clone.1 | convolution fusion | flops 4345290752 | bytes 74481664 | tf_op jit(solution)/shard_map/while/body/eval_jaxpr/bqkgd,bskd->bkgqs/dot_general | solution.py:52
  457.8 21.5 fusion.141
  479.3 29.6 %bitcast_dynamic-update-slice_fusion.6 = bf16[4,8,512,1,2,128]{5,2,0,4,1,3:T(8,128)(2,1)} fusion(bf16[4,8,512,1,2,128]{5,2,0,4,1,3:T(8,128)(2,1)} %get-tuple-element.368, s32[]{:T(128)S(6)} %copy.394, bf16[8,2048,1,128]{3,1,0,2:T(8,128)(2,1)} %get-tuple-element.384, f32[8,2,512]{2,1,0:T(2,128)S(1)} %fusion.141, ...), kind=kOutput, calls=%fused_computation.13.clone.1 | convolution fusion | flops 4379901952 | bytes 74514432 | tf_op jit(solution)/shard_map/while/body/eval_jaxpr/bkgqs,bskd->bqkgd/dot_general | solution.py:59
  510.9 26.1 %fusion.140 = (f32[8,2,512]{2,1,0:T(2,128)S(1)}, f32[8,512,2,2048]{3,1,2,0:T(8,128)}) fusion(pred[512,2048]{1,0:T(8,128)(4,1)S(1)} %iota_compare_fusion.4, bf16[8,2048,1,128]{3,1,0,2:T(8,128)(2,1)} %get-tuple-element.383, bf16[8,2048,1,2,128]{4,1,3,0,2:T(8,128)(2,1)} %get-tuple-element.382, s32[]{:T(128)S(6)} %select_n.64), kind=kOutput, calls=%fused_computation.6.clone.1 | convolution fusion | flops 4345290752 | bytes 74481664 | tf_op jit(solution)/shard_map/while/body/eval_jaxpr/bqkgd,bskd->bkgqs/dot_general | solution.py:52
  536.9 21.5 fusion.141
  558.5 29.6 %bitcast_dynamic-update-slice_fusion.6 = bf16[4,8,512,1,2,128]{5,2,0,4,1,3:T(8,128)(2,1)} fusion(bf16[4,8,512,1,2,128]{5,2,0,4,1,3:T(8,128)(2,1)} %get-tuple-element.368, s32[]{:T(128)S(6)} %copy.394, bf16[8,2048,1,128]{3,1,0,2:T(8,128)(2,1)} %get-tuple-element.384, f32[8,2,512]{2,1,0:T(2,128)S(1)} %fusion.141, ...), kind=kOutput, calls=%fused_computation.13.clone.1 | convolution fusion | flops 4379901952 | bytes 74514432 | tf_op jit(solution)/shard_map/while/body/eval_jaxpr/bkgqs,bskd->bqkgd/dot_general | solution.py:59
  590.1 26.1 %fusion.140 = (f32[8,2,512]{2,1,0:T(2,128)S(1)}, f32[8,512,2,2048]{3,1,2,0:T(8,128)}) fusion(pred[512,2048]{1,0:T(8,128)(4,1)S(1)} %iota_compare_fusion.4, bf16[8,2048,1,128]{3,1,0,2:T(8,128)(2,1)} %get-tuple-element.383, bf16[8,2048,1,2,128]{4,1,3,0,2:T(8,128)(2,1)} %get-tuple-element.382, s32[]{:T(128)S(6)} %select_n.64), kind=kOutput, calls=%fused_computation.6.clone.1 | convolution fusion | flops 4345290752 | bytes 74481664 | tf_op jit(solution)/shard_map/while/body/eval_jaxpr/bqkgd,bskd->bkgqs/dot_general | solution.py:52
  616.1 21.5 fusion.141
  637.7 29.6 %bitcast_dynamic-update-slice_fusion.6 = bf16[4,8,512,1,2,128]{5,2,0,4,1,3:T(8,128)(2,1)} fusion(bf16[4,8,512,1,2,128]{5,2,0,4,1,3:T(8,128)(2,1)} %get-tuple-element.368, s32[]{:T(128)S(6)} %copy.394, bf16[8,2048,1,128]{3,1,0,2:T(8,128)(2,1)} %get-tuple-element.384, f32[8,2,512]{2,1,0:T(2,128)S(1)} %fusion.141, ...), kind=kOutput, calls=%fused_computation.13.clone.1 | convolution fusion | flops 4379901952 | bytes 74514432 | tf_op jit(solution)/shard_map/while/body/eval_jaxpr/bkgqs,bskd->bqkgd/dot_general | solution.py:59
  680.9 558.7 %while.29 = (s32[]{:T(128)}, f32[8,2048,1,128]{1,3,0,2:T(8,128)}, f32[8,2048,1,128]{1,3,0,2:T(8,128)}, bf16[4,8,512,1,2,128]{5,2,0,4,1,3:T(8,128)(2,1)}, s32[4]{...) while((s32[]{:T(128)}, f32[8,2048,1,128]{1,3,0,2:T(8,128)}, ...), condition=%wide.region_6.7_spmd.clone, body=%wide.region_5.6_spmd.clone.sunk | while | flops 21669871616 | bytes 361992448 | solution.py:94
  684.9 26.7 %fusion.152 = f32[8,512,2,2048]{3,1,2,0:T(8,128)} fusion(bf16[8,2048,1,128]{3,1,0,2:T(8,128)(2,1)} %get-tuple-element.427, bf16[8,2048,1,2,128]{4,1,3,0,2:T(8,128)(2,1)} %get-tuple-element.426, s32[]{:T(128)S(6)} %select_n.67), kind=kOutput, calls=%fused_computation.38.clone.1 | convolution fusion | flops 4294967296 | bytes 73400320 | tf_op jit(solution)/shard_map/while/body/eval_jaxpr/bqkgd,bskd->bkgqs/dot_general | solution.py:81
  711.7 29.2 %bitcast_add_fusion.5 = f32[8,2048,1,128]{1,3,0,2:T(8,128)} fusion(f32[8,2048,1,128]{1,3,0,2:T(8,128)} %get-tuple-element.407, f32[8,512,2,2048]{3,1,2,0:T(8,128)} %fusion.152, f32[8,2,512]{2,1,0:T(2,128)S(1)} %dynamic-slice_bitcast_fusion.5, pred[512,2048]{1,0:T(8,128)(4,1)S(1)} %iota_compare_fusion.5, pred[]{:T(512)S(6)} %compare.3, ...), kind=kOutput, calls=%fused_computation.33.clone.1 | convolution fusion | flops 4366270464 | bytes 87064584 | tf_op jit(solution)/shard_map/while/body/eval_jaxpr/bkgqs,bqkgd->bskd/dot_general | solution.py:87
  740.8 42.0 %fusion.153 = bf16[8,2,512,2048]{3,2,1,0:T(8,128)(2,1)} fusion(f32[8,512,2,2048]{3,1,2,0:T(8,128)} %fusion.152, f32[8,2,512]{2,1,0:T(2,128)S(1)} %dynamic-slice_bitcast_fusion.4, f32[8,2,512]{2,1,0:T(2,128)S(1)} %dynamic-slice_bitcast_fusion.5, pred[512,2048]{1,0:T(8,128)(4,1)S(1)} %iota_compare_fusion.5, ...), kind=kOutput, calls=%fused_computation.30.clone.2 | convolution fusion | flops 4412407808 | bytes 108068864 | tf_op jit(solution)/shard_map/while/body/eval_jaxpr/bqkgd,bskd->bkgqs/dot_general | solution.py:85
  782.8 17.4 bitcast_add_fusion.4
  821.4 26.7 %fusion.152 = f32[8,512,2,2048]{3,1,2,0:T(8,128)} fusion(bf16[8,2048,1,128]{3,1,0,2:T(8,128)(2,1)} %get-tuple-element.427, bf16[8,2048,1,2,128]{4,1,3,0,2:T(8,128)(2,1)} %get-tuple-element.426, s32[]{:T(128)S(6)} %select_n.67), kind=kOutput, calls=%fused_computation.38.clone.1 | convolution fusion | flops 4294967296 | bytes 73400320 | tf_op jit(solution)/shard_map/while/body/eval_jaxpr/bqkgd,bskd->bkgqs/dot_general | solution.py:81
  848.1 30.9 %bitcast_add_fusion.5 = f32[8,2048,1,128]{1,3,0,2:T(8,128)} fusion(f32[8,2048,1,128]{1,3,0,2:T(8,128)} %get-tuple-element.407, f32[8,512,2,2048]{3,1,2,0:T(8,128)} %fusion.152, f32[8,2,512]{2,1,0:T(2,128)S(1)} %dynamic-slice_bitcast_fusion.5, pred[512,2048]{1,0:T(8,128)(4,1)S(1)} %iota_compare_fusion.5, pred[]{:T(512)S(6)} %compare.3, ...), kind=kOutput, calls=%fused_computation.33.clone.1 | convolution fusion | flops 4366270464 | bytes 87064584 | tf_op jit(solution)/shard_map/while/body/eval_jaxpr/bkgqs,bqkgd->bskd/dot_general | solution.py:87
  879.1 42.0 %fusion.153 = bf16[8,2,512,2048]{3,2,1,0:T(8,128)(2,1)} fusion(f32[8,512,2,2048]{3,1,2,0:T(8,128)} %fusion.152, f32[8,2,512]{2,1,0:T(2,128)S(1)} %dynamic-slice_bitcast_fusion.4, f32[8,2,512]{2,1,0:T(2,128)S(1)} %dynamic-slice_bitcast_fusion.5, pred[512,2048]{1,0:T(8,128)(4,1)S(1)} %iota_compare_fusion.5, ...), kind=kOutput, calls=%fused_computation.30.clone.2 | convolution fusion | flops 4412407808 | bytes 108068864 | tf_op jit(solution)/shard_map/while/body/eval_jaxpr/bqkgd,bskd->bkgqs/dot_general | solution.py:85
  921.0 19.8 bitcast_add_fusion.4
  940.8 17.3 bitcast_dynamic-update-slice_fusion.8
  962.0 26.7 %fusion.152 = f32[8,512,2,2048]{3,1,2,0:T(8,128)} fusion(bf16[8,2048,1,128]{3,1,0,2:T(8,128)(2,1)} %get-tuple-element.427, bf16[8,2048,1,2,128]{4,1,3,0,2:T(8,128)(2,1)} %get-tuple-element.426, s32[]{:T(128)S(6)} %select_n.67), kind=kOutput, calls=%fused_computation.38.clone.1 | convolution fusion | flops 4294967296 | bytes 73400320 | tf_op jit(solution)/shard_map/while/body/eval_jaxpr/bqkgd,bskd->bkgqs/dot_general | solution.py:81
  988.7 30.9 %bitcast_add_fusion.5 = f32[8,2048,1,128]{1,3,0,2:T(8,128)} fusion(f32[8,2048,1,128]{1,3,0,2:T(8,128)} %get-tuple-element.407, f32[8,512,2,2048]{3,1,2,0:T(8,128)} %fusion.152, f32[8,2,512]{2,1,0:T(2,128)S(1)} %dynamic-slice_bitcast_fusion.5, pred[512,2048]{1,0:T(8,128)(4,1)S(1)} %iota_compare_fusion.5, pred[]{:T(512)S(6)} %compare.3, ...), kind=kOutput, calls=%fused_computation.33.clone.1 | convolution fusion | flops 4366270464 | bytes 87064584 | tf_op jit(solution)/shard_map/while/body/eval_jaxpr/bkgqs,bqkgd->bskd/dot_general | solution.py:87
  1019.6 42.0 %fusion.153 = bf16[8,2,512,2048]{3,2,1,0:T(8,128)(2,1)} fusion(f32[8,512,2,2048]{3,1,2,0:T(8,128)} %fusion.152, f32[8,2,512]{2,1,0:T(2,128)S(1)} %dynamic-slice_bitcast_fusion.4, f32[8,2,512]{2,1,0:T(2,128)S(1)} %dynamic-slice_bitcast_fusion.5, pred[512,2048]{1,0:T(8,128)(4,1)S(1)} %iota_compare_fusion.5, ...), kind=kOutput, calls=%fused_computation.30.clone.2 | convolution fusion | flops 4412407808 | bytes 108068864 | tf_op jit(solution)/shard_map/while/body/eval_jaxpr/bqkgd,bskd->bkgqs/dot_general | solution.py:85
  1061.6 19.8 bitcast_add_fusion.4
  1081.4 17.3 bitcast_dynamic-update-slice_fusion.8
  1102.6 26.7 %fusion.152 = f32[8,512,2,2048]{3,1,2,0:T(8,128)} fusion(bf16[8,2048,1,128]{3,1,0,2:T(8,128)(2,1)} %get-tuple-element.427, bf16[8,2048,1,2,128]{4,1,3,0,2:T(8,128)(2,1)} %get-tuple-element.426, s32[]{:T(128)S(6)} %select_n.67), kind=kOutput, calls=%fused_computation.38.clone.1 | convolution fusion | flops 4294967296 | bytes 73400320 | tf_op jit(solution)/shard_map/while/body/eval_jaxpr/bqkgd,bskd->bkgqs/dot_general | solution.py:81
  1129.3 30.9 %bitcast_add_fusion.5 = f32[8,2048,1,128]{1,3,0,2:T(8,128)} fusion(f32[8,2048,1,128]{1,3,0,2:T(8,128)} %get-tuple-element.407, f32[8,512,2,2048]{3,1,2,0:T(8,128)} %fusion.152, f32[8,2,512]{2,1,0:T(2,128)S(1)} %dynamic-slice_bitcast_fusion.5, pred[512,2048]{1,0:T(8,128)(4,1)S(1)} %iota_compare_fusion.5, pred[]{:T(512)S(6)} %compare.3, ...), kind=kOutput, calls=%fused_computation.33.clone.1 | convolution fusion | flops 4366270464 | bytes 87064584 | tf_op jit(solution)/shard_map/while/body/eval_jaxpr/bkgqs,bqkgd->bskd/dot_general | solution.py:87
  1160.2 42.0 %fusion.153 = bf16[8,2,512,2048]{3,2,1,0:T(8,128)(2,1)} fusion(f32[8,512,2,2048]{3,1,2,0:T(8,128)} %fusion.152, f32[8,2,512]{2,1,0:T(2,128)S(1)} %dynamic-slice_bitcast_fusion.4, f32[8,2,512]{2,1,0:T(2,128)S(1)} %dynamic-slice_bitcast_fusion.5, pred[512,2048]{1,0:T(8,128)(4,1)S(1)} %iota_compare_fusion.5, ...), kind=kOutput, calls=%fused_computation.30.clone.2 | convolution fusion | flops 4412407808 | bytes 108068864 | tf_op jit(solution)/shard_map/while/body/eval_jaxpr/bqkgd,bskd->bkgqs/dot_general | solution.py:85
  1202.2 19.8 bitcast_add_fusion.4
  1222.0 17.3 bitcast_dynamic-update-slice_fusion.8
  1269.0 84.7 %all-to-all-done.5 = bf16[8,2048,2,128]{3,2,0,1:T(2,128)(2,1)} async-done(((bf16[8,2048,2,128]{3,2,0,1:T(2,128)(2,1)}), bf16[8,2048,2,128]{3,2,0,1:T(2,128)(2,1)}, u32[]{:S(2)}, u32[]{:S(2)}) %all-to-all-start.5) | async-done | bytes 8388640 | tf_op jit(solution)/shard_map/all_to_all | solution.py:142
  1366.8 84.7 %all-to-all-done.6 = f32[8,2048,1,128]{3,0,2,1:T(8,128)} async-done(((f32[8,2048,1,128]{3,0,2,1:T(8,128)}), f32[8,2048,1,128]{3,0,2,1:T(8,128)}, u32[]{:S(2)}, u32[]{:S(2)}) %all-to-all-start.6) | async-done | bytes 8388640 | tf_op jit(solution)/shard_map/all_to_all | solution.py:144
  1471.7 77.6 %all-to-all-done.7 = f32[8,2048,1,128]{3,0,2,1:T(8,128)} async-done(((f32[8,2048,1,128]{3,0,2,1:T(8,128)}), f32[8,2048,1,128]{3,0,2,1:T(8,128)}, u32[]{:S(2)}, u32[]{:S(2)}) %all-to-all-start.7) | async-done | bytes 8388640 | tf_op jit(solution)/shard_map/all_to_all | solution.py:145
  1700.1 24.4 %convolution_bitcast_fusion = f32[2048,2048]{1,0:T(8,128)} fusion(bf16[8,256,2048]{2,1,0:T(8,128)(2,1)} %reshape.215, bf16[8,256,2048]{2,1,0:T(8,128)(2,1)} %param.16), kind=kOutput, calls=%fused_computation.84 | convolution fusion | flops 17179869184 | bytes 33554432 | tf_op jit(solution)/shard_map/btd,bte->de/dot_general | solution.py:135
  1724.5 19.7 multiply_subtract_fusion
  1760.3 26.2 %convolution_bitcast_fusion.1 = f32[2048,2048]{1,0:T(8,128)} fusion(bf16[8,16,32,8,128]{4,3,2,1,0:T(8,128)(2,1)} %convert_bitcast_fusion.1, bf16[8,256,2048]{2,1,0:T(8,128)(2,1)} %param.15, f32[2048]{0:T(1024)S(1)} %copy-done.16, f32[8,256]{1,0:T(8,128)S(1)} %copy-done.18), kind=kOutput, calls=%fused_computation.85 | convolution fusion | flops 17196646400 | bytes 33570816 | tf_op jit(solution)/shard_map/btd,bte->de/dot_general | solution.py:156
  1820.9 30.8 %fusion.64 = (f32[2048]{0:T(1024)S(1)}, f32[8,256]{1,0:T(8,128)S(1)}, f32[8,256,2048]{2,1,0:T(8,128)}) fusion(bf16[8,256,2048]{2,1,0:T(8,128)(2,1)} %param.15, f32[8,256]{1,0:T(8,128)S(1)} %copy-done.18, f32[2048]{0:T(1024)S(1)} %copy-done.16, f32[8,256,2048]{2,1,0:T(8,128)} %fusion.91, f32[8,256,2048]{2,1,0:T(8,128)} %fusion.94, ...), kind=kOutput, calls=%fused_computation.72 | convolution fusion | flops 17217613824 | bytes 75530240 | tf_op jit(solution)/shard_map/bte,de->btd/dot_general | solution.py:159
  1851.7 24.8 %all-reduce = (f32[2048]{0:T(1024)}, f32[2048]{0:T(1024)}, f32[256]{0:T(256)}, f32[256]{0:T(256)}) all-reduce(f32[2048]{0:T(1024)S(1)} %get-tuple-element.176, f32[2048]{0:T(1024)S(1)} %bitcast.372, f32[256]{0:T(256)S(1)} %bitcast.374, f32[256]{0:T(256)S(1)} %bitcast.375), channel_id=1, replica_groups=mesh['dp'=1,'sp'=8] {'sp'}, use_global_device_ids=true, to_apply=%region_11.12 | all-reduce | flops 4608 | bytes 36864 | tf_op jit(solution)/shard_map/psum | solution.py:164
  1891.4 25.0 %fusion.66 = bf16[8,256,2048]{2,1,0:T(8,128)(2,1)} fusion(bf16[8,256,2048]{2,1,0:T(8,128)(2,1)} %param.15, bf16[8,256,2048]{2,1,0:T(8,128)(2,1)} %reshape.215, bf16[2048,2048]{1,0:T(8,128)(2,1)} %param.25), kind=kOutput, calls=%fused_computation.74 | convolution fusion | flops 17192452096 | bytes 33554432 | tf_op jit(solution)/shard_map/btd,de->bte/dot_general | solution.py:132
  1916.4 305.8 %all-reduce.4.cloned.1.call-done = (f32[2048,2048]{1,0:T(8,128)}, f32[2048,256]{1,0:T(8,128)}, f32[2048,256]{1,0:T(8,128)}, f32[2048,2048]{1,0:T(8,128)}) async-done(((f32[2048,2048]{1,0:T(8,128)}, f32[2048,256]{1,0:T(8,128)}, f32[2048,256]{1,0:T(8,128)}, f32[2048,2048]{1,0:T(8,128)}), (f32[2048,2048]{1,0:T(8,128)}, f32[2048,256]{1,0:T(8,128)}, f32[2048,256]{1,0:T(8,128)}, ...) | async-done | bytes 37748752 | tf_op jit(solution)/shard_map/psum | solution.py:164
  (178 shorter events, 501.3 us)
Async XLA Ops:
  7.2 29.7 %copy-start = (bf16[2048,256]{1,0:T(8,128)(2,1)S(1)}, bf16[2048,256]{1,0:T(8,128)(2,1)}, u32[]{:S(2)}) copy-start(bf16[2048,256]{1,0:T(8,128)(2,1)} %param.23) | copy-start | bytes 3145732
  7.2 7.8 copy-start.2
  8.9 136.1 %copy-start.15 = (f32[2048]{0:T(1024)}, f32[2048]{0:T(1024)S(1)}, u32[]{:S(2)}) copy-start(f32[2048]{0:T(1024)S(1)} %convert_element_type.104) | copy-start | bytes 24580
  15.0 130.0 %copy-start.17 = (f32[8,256]{1,0:T(8,128)}, f32[8,256]{1,0:T(8,128)S(1)}, u32[]{:S(2)}) copy-start(f32[8,256]{1,0:T(8,128)S(1)} %add_rsqrt_fusion) | copy-start | bytes 24580
  22.2 147.3 %copy-start.5 = (f32[8,256,64]{1,2,0:T(8,128)}, f32[8,256,64]{1,2,0:T(8,128)S(1)}, u32[]{:S(2)}) copy-start(f32[8,256,64]{1,2,0:T(8,128)S(1)} %get-tuple-element.240) | copy-start | bytes 1572868
  26.4 10.5 copy-start.20
  31.9 53.9 %all-to-all-start.1 = ((bf16[8,256,8,128]{3,1,0,2:T(8,128)(2,1)}), bf16[8,256,8,128]{3,1,0,2:T(8,128)(2,1)}, u32[]{:S(2)}, u32[]{:S(2)}) async-start(bf16[8,256,8,128]{3,1,0,2:T(8,128)(2,1)} %bitcast.361), calls=%async_computation.1 | async-start | bytes 8388608 | tf_op jit(solution)/shard_map/all_to_all | solution.py:127
  43.9 48.3 %copy-start.19 = (bf16[2048]{0:T(1024)(128)(2,1)S(1)}, bf16[2048]{0:T(1024)(128)(2,1)}, u32[]{:S(2)}) copy-start(bf16[2048]{0:T(1024)(128)(2,1)} %param.20) | copy-start | bytes 12292
  88.9 52.3 %all-to-all-start.2 = ((bf16[8,256,8,128]{3,1,0,2:T(8,128)(2,1)}), bf16[8,256,8,128]{3,1,0,2:T(8,128)(2,1)}, u32[]{:S(2)}, u32[]{:S(2)}) async-start(bf16[8,256,8,128]{3,1,0,2:T(8,128)(2,1)} %bitcast.362), calls=%async_computation.2 | async-start | bytes 8388608 | tf_op jit(solution)/shard_map/all_to_all | solution.py:128
  141.2 97.9 %all-to-all-start.4 = ((bf16[8,256,16,128]{3,1,0,2:T(8,128)(2,1)}), bf16[8,256,16,128]{3,1,0,2:T(8,128)(2,1)}, u32[]{:S(2)}, u32[]{:S(2)}) async-start(bf16[8,256,16,128]{3,1,0,2:T(8,128)(2,1)} %bitcast.358), calls=%async_computation.4 | async-start | bytes 16777216 | tf_op jit(solution)/shard_map/all_to_all | solution.py:137
  169.8 23.1 %copy-start.3 = (f32[8,256,64]{2,1,0:T(8,128)}, f32[8,256,64]{2,1,0:T(8,128)S(1)}, u32[]{:S(2)}) copy-start(f32[8,256,64]{2,1,0:T(8,128)S(1)} %copy.285) | copy-start | bytes 1572868
  180.6 12.3 copy-start.11
  239.0 97.8 %all-to-all-start = ((bf16[8,256,16,128]{3,1,0,2:T(8,128)(2,1)}), bf16[8,256,16,128]{3,1,0,2:T(8,128)(2,1)}, u32[]{:S(2)}, u32[]{:S(2)}) async-start(bf16[8,256,16,128]{3,1,0,2:T(8,128)(2,1)} %copy.288), calls=%async_computation | async-start | bytes 16777216 | tf_op jit(solution)/shard_map/all_to_all | solution.py:126
  1256.1 97.7 %all-to-all-start.5 = ((bf16[8,2048,2,128]{3,2,0,1:T(2,128)(2,1)}), bf16[8,2048,2,128]{3,2,0,1:T(2,128)(2,1)}, u32[]{:S(2)}, u32[]{:S(2)}) async-start(bf16[8,2048,2,128]{3,2,0,1:T(2,128)(2,1)} %copy.307), calls=%async_computation.5 | async-start | bytes 16777216 | tf_op jit(solution)/shard_map/all_to_all | solution.py:142
  1353.7 97.8 %all-to-all-start.6 = ((f32[8,2048,1,128]{3,0,2,1:T(8,128)}), f32[8,2048,1,128]{3,0,2,1:T(8,128)}, u32[]{:S(2)}, u32[]{:S(2)}) async-start(f32[8,2048,1,128]{3,0,2,1:T(8,128)} %copy.312), calls=%async_computation.6 | async-start | bytes 16777216 | tf_op jit(solution)/shard_map/all_to_all | solution.py:144
  1451.5 97.8 %all-to-all-start.7 = ((f32[8,2048,1,128]{3,0,2,1:T(8,128)}), f32[8,2048,1,128]{3,0,2,1:T(8,128)}, u32[]{:S(2)}, u32[]{:S(2)}) async-start(f32[8,2048,1,128]{3,0,2,1:T(8,128)} %copy.315), calls=%async_computation.7 | async-start | bytes 16777216 | tf_op jit(solution)/shard_map/all_to_all | solution.py:145
  1471.7 81.3 %copy-start.10 = (f32[8,256,64]{1,2,0:T(8,128)S(1)}, f32[8,256,64]{1,2,0:T(8,128)}, u32[]{:S(2)}) copy-start(f32[8,256,64]{1,2,0:T(8,128)} %get-tuple-element.238) | copy-start | bytes 1572868
  1549.3 111.0 %all-to-all-start.3 = ((bf16[8,2048,2,128]{3,2,0,1:T(2,128)(2,1)}), bf16[8,2048,2,128]{3,2,0,1:T(2,128)(2,1)}, u32[]{:S(2)}, u32[]{:S(2)}) async-start(bf16[8,2048,2,128]{3,2,0,1:T(2,128)(2,1)} %copy.299), calls=%async_computation.3 | async-start | bytes 16777216 | tf_op jit(solution)/shard_map/all_to_all | solution.py:130
  1553.0 669.2 %all-reduce.4.cloned.1.call-start = ((), (), s32[]{:S(2)}) async-start(), calls=%async_computation.8 | async-start | bytes 75497472 | tf_op jit(solution)/shard_map/psum | solution.py:164
  1631.6 12.1 copy-start.16
  1631.6 12.1 copy-start.18
  1643.7 8.4 copy-start.8
  1643.7 8.4 copy-start.6
  1700.1 24.4 %copy-start.4 = (f32[8,256,64]{2,1,0:T(8,128)S(1)}, f32[8,256,64]{2,1,0:T(8,128)}, u32[]{:S(2)}) copy-start(f32[8,256,64]{2,1,0:T(8,128)} %copy-done.3) | copy-start | bytes 1572868
  1744.2 16.1 copy-start.1
  1791.5 12.3 copy-start.9
  1803.8 8.6 copy-start.7
  1803.8 8.6 copy-start.14
  2222.2 16.4 slice-start
  2222.2 13.8 copy-start.13
  2222.2 15.1 copy-start.12
  2222.2 16.4 slice-start.1
  2222.2 18.1 slice-start.2
  2222.2 19.3 slice-start.3
Sparse Core Ops, SparseCore 0:
  1786.7 435.4 all-reduce.3
where the time goes:
time: 2260 us; the launch traced here: 2250 us
  matrix products  965 us (43%)
  waiting for transfers between devices  697 us (31%)
  local copies, waits for them, and re-layouts  268 us (12%)
  other arithmetic  241 us (11%)
  starting transfers between devices  30.8 us (1%)
  blocking collectives  24.8 us (1%)
    psum x1, waiting for transfers between devices, device_step(): lax.psum((jnp.sum(gain_terms, axis=(0, 1)), d_w_query, jnp.sum(dq_pre, ax...  306 us
    dot_general x8, matrix products, one_block(): jnp.einsum('bqkgd,bskd->bkgqs', q_block, keys, preferred_element_type=jnp...  211 us
    dot_general x4, matrix products, one_block(): jnp.einsum('bqkgd,bskd->bkgqs', do_block, values, preferred_element_type=...  168 us
    dot_general x4, matrix products, one_block(): jnp.einsum('bkgqs,bqkgd->bskd', probs.astype(jnp.bfloat16), do_block, pre...  122 us
    dot_general x4, matrix products, one_block(): jnp.einsum('bkgqs,bskd->bqkgd', probs, values, preferred_element_type=jnp...  119 us
    reduce_sum x4, other arithmetic, one_block(): total = jnp.sum(exp_scores, axis=-1, keepdims=True)  86.1 us
    all_to_all x1, waiting for transfers between devices, device_step(): d_keys = lax.all_to_all(dk_h.astype(wire_type), 'sp', 1, 2, tiled=True)  84.7 us
    all_to_all x1, waiting for transfers between devices, device_step(): lax.all_to_all(dq_h.reshape(batch, seq, heads_local, HEAD_DIM), 'sp', 1,...  84.7 us
  transfers between devices with their start and end apart: 9, of which 8 were waited for; matrix products, arithmetic and copies ran while one was open for 17% of the time, Pallas kernels for 0%

commit v1 on v0

v1 whole, which is shorter than its diff:
```python
import functools
import math
import jax
import jax.numpy as jnp
from jax import lax
from jax.experimental import pallas as pl
from jax.experimental.pallas import tpu as pltpu
from jax.sharding import PartitionSpec as P

HEAD_DIM = 128
HALF = HEAD_DIM // 2
ROPE_BASE = 1000000.0
NORM_EPS = 1e-6
SCALE = HEAD_DIM ** -0.5
EXP2_SCALE = SCALE * math.log2(math.e)
MASKED = -1e30
NT_DIMS = (((1,), (1,)), ((), ()))


def dot_nt(left, right):
    return lax.dot_general(left, right, NT_DIMS, preferred_element_type=jnp.float32)


def dot_nn(left, right):
    return jnp.dot(left, right, preferred_element_type=jnp.float32)


def head_cols(head):
    return slice(head * HEAD_DIM, (head + 1) * HEAD_DIM)


def attn_fwd_kernel(index_ref, q_ref, do_ref, kv_ref, out_ref, lse_ref, delta_ref, v_t, peak, total, acc):
    index = index_ref[0]
    heads = q_ref.shape[1] // HEAD_DIM
    blocks, _, block, _ = kv_ref.shape
    pair = 2 * block

    for j in range(blocks):
        v_t[j] = kv_ref[j, 0, :, HEAD_DIM:].T
    peak[...] = jnp.full(peak.shape, MASKED, jnp.float32)
    total[...] = jnp.zeros(total.shape, jnp.float32)
    acc[...] = jnp.zeros(acc.shape, jnp.float32)

    def step(number, masked):
        keys = kv_ref[pl.ds(2 * number, 2), 0, :, :HEAD_DIM].reshape(pair, HEAD_DIM)
        if masked:
            key_pos = number * pair + lax.broadcasted_iota(jnp.int32, (pair, block), 0)
            query_pos = index * block + lax.broadcasted_iota(jnp.int32, (pair, block), 1)
            keep = key_pos <= query_pos
        scores_next = dot_nt(keys, q_ref[:, head_cols(0)])
        for h in range(heads):
            scores = scores_next
            if h + 1 < heads:
                scores_next = dot_nt(keys, q_ref[:, head_cols(h + 1)])
            if masked:
                scores = jnp.where(keep, scores, MASKED)
            old_peak = peak[h:h + 1, :]
            new_peak = jnp.maximum(old_peak, jnp.max(scores, axis=0, keepdims=True))
            alpha = jnp.exp2((old_peak - new_peak) * EXP2_SCALE)
            probs = jnp.exp2(scores * EXP2_SCALE - new_peak * EXP2_SCALE)
            total[h:h + 1, :] = alpha * total[h:h + 1, :] + jnp.sum(probs, axis=0, keepdims=True)
            peak[h:h + 1, :] = new_peak
            probs = probs.astype(jnp.bfloat16)
            update = dot_nn(v_t[2 * number], probs[:block]) + dot_nn(v_t[2 * number + 1], probs[block:])
            acc[h] = acc[h] * alpha + update

    full = index // 2

    @pl.loop(0, full)
    def _(number):
        step(number, False)

    step(full, True)

    for h in range(heads):
        out_t = (acc[h] / total[h:h + 1, :]).astype(jnp.bfloat16)
        out_ref[:, head_cols(h)] = out_t.T
        do_t = do_ref[:, head_cols(h)].T
        delta_ref[0, h:h + 1, :] = jnp.sum(out_t.astype(jnp.float32) * do_t.astype(jnp.float32), axis=0, keepdims=True)
    lse_ref[0] = peak[...] * EXP2_SCALE + jnp.log2(total[...])


def attn_bwd_kernel(index_ref, q_ref, do_ref, kv_ref, lse_ref, delta_ref, cos_ref, sin_ref,
                    dq_ref, dbq_ref, dkv_ref, dq_t):
    index = index_ref[0]
    heads = q_ref.shape[1] // HEAD_DIM
    blocks, _, block, _ = kv_ref.shape
    dq_t[...] = jnp.zeros(dq_t.shape, jnp.float32)

    def step(j, masked):
        keys = kv_ref[j, 0, :, :HEAD_DIM]
        values = kv_ref[j, 0, :, HEAD_DIM:]
        keys_t = keys.T
        d_keys = jnp.zeros((block, HEAD_DIM), jnp.float32)
        d_values = jnp.zeros((block, HEAD_DIM), jnp.float32)
        if masked:
            keep = (lax.broadcasted_iota(jnp.int32, (block, block), 0)
                    <= lax.broadcasted_iota(jnp.int32, (block, block), 1))
        for h in range(heads):
            query = q_ref[:, head_cols(h)]
            d_out = do_ref[:, head_cols(h)]
            scores = dot_nt(keys, query)
            d_probs = dot_nt(values, d_out)
            if masked:
                scores = jnp.where(keep, scores, MASKED)
            probs = jnp.exp2(scores * EXP2_SCALE - lse_ref[0, h:h + 1, :])
            d_scores = (probs * (d_probs - delta_ref[0, h:h + 1, :])).astype(jnp.bfloat16)
            d_values += dot_nn(probs.astype(jnp.bfloat16), d_out)
            d_keys += dot_nn(d_scores, query)
            dq_t[h] += dot_nn(keys_t, d_scores)
        dkv_ref[j, 0, :, :HEAD_DIM] = d_keys * SCALE
        dkv_ref[j, 0, :, HEAD_DIM:] = d_values

    @pl.loop(0, index)
    def _(j):
        step(j, False)

    step(index, True)

    @pl.loop(index + 1, blocks)
    def _(j):
        dkv_ref[j, 0] = jnp.zeros(dkv_ref.shape[2:], jnp.float32)

    @pl.when(pl.program_id(0) == 0)
    def _():
        dbq_ref[...] = jnp.zeros(dbq_ref.shape, jnp.float32)

    cosine = cos_ref[0]
    sine = sin_ref[0]
    for h in range(heads):
        first = dq_t[h, :HALF, :] * SCALE
        second = dq_t[h, HALF:, :] * SCALE
        dq_pre = jnp.concatenate([first * cosine + second * sine, second * cosine - first * sine], axis=0).T
        dbq_ref[:, head_cols(h)] += jnp.sum(dq_pre, axis=0, keepdims=True)
        dq_ref[:, head_cols(h)] = dq_pre.astype(jnp.bfloat16)


def attn_sizes(query, kv_all, kv_heads):
    blocks, batch, block, _ = kv_all.shape
    width = query.shape[1] // kv_heads
    return blocks, batch, block, width, width // HEAD_DIM


def attn_forward(index, query, d_att, kv_all, kv_head, kv_heads):
    blocks, batch, block, width, heads = attn_sizes(query, kv_all, kv_heads)
    cols = pl.BlockSpec((block, width), lambda b, _: (b, kv_head))
    stats = pl.BlockSpec((1, heads, block), lambda b, _: (b, 0, 0))
    stats_shape = jax.ShapeDtypeStruct((batch, heads, block), jnp.float32)
    grid_spec = pltpu.PrefetchScalarGridSpec(
        num_scalar_prefetch=1, grid=(batch,),
        in_specs=[cols, cols, pl.BlockSpec((blocks, 1, block, 2 * HEAD_DIM), lambda b, _: (0, b, 0, 0))],
        out_specs=[pl.BlockSpec((block, width), lambda b, _: (b, 0)), stats, stats],
        scratch_shapes=[pltpu.VMEM((blocks, HEAD_DIM, block), jnp.bfloat16),
                        pltpu.VMEM((heads, block), jnp.float32), pltpu.VMEM((heads, block), jnp.float32),
                        pltpu.VMEM((heads, HEAD_DIM, block), jnp.float32)])
    work = batch * heads * block * block * blocks
    return pl.pallas_call(
        attn_fwd_kernel, grid_spec=grid_spec,
        out_shape=[jax.ShapeDtypeStruct((batch * block, width), jnp.bfloat16), stats_shape, stats_shape],
        compiler_params=pltpu.CompilerParams(dimension_semantics=("arbitrary",)),
        cost_estimate=pl.CostEstimate(flops=8 * work * HEAD_DIM, bytes_accessed=2 ** 24, transcendentals=work),
        name="attn_fwd")(index, query, d_att, kv_all)


def attn_backward(index, query, d_att, kv_all, lse, delta, cos_t, sin_t, kv_head, kv_heads):
    blocks, batch, block, width, heads = attn_sizes(query, kv_all, kv_heads)
    cols = pl.BlockSpec((block, width), lambda b, _: (b, kv_head))
    stats = pl.BlockSpec((1, heads, block), lambda b, _: (b, 0, 0))
    table = pl.BlockSpec((1, HALF, block), lambda b, _: (b, 0, 0))
    all_keys = pl.BlockSpec((blocks, 1, block, 2 * HEAD_DIM), lambda b, _: (0, b, 0, 0))
    grid_spec = pltpu.PrefetchScalarGridSpec(
        num_scalar_prefetch=1, grid=(batch,),
        in_specs=[cols, cols, all_keys, stats, stats, table, table],
        out_specs=[pl.BlockSpec((block, width), lambda b, _: (b, 0)),
                   pl.BlockSpec((1, width), lambda b, _: (0, 0)), all_keys],
        scratch_shapes=[pltpu.VMEM((heads, HEAD_DIM, block), jnp.float32)])
    work = batch * heads * block * block * blocks
    return pl.pallas_call(
        attn_bwd_kernel, grid_spec=grid_spec,
        out_shape=[jax.ShapeDtypeStruct((batch * block, width), jnp.bfloat16),
                   jax.ShapeDtypeStruct((1, width), jnp.float32),
                   jax.ShapeDtypeStruct(kv_all.shape, jnp.float32)],
        compiler_params=pltpu.CompilerParams(dimension_semantics=("arbitrary",)),
        cost_estimate=pl.CostEstimate(flops=20 * work * HEAD_DIM, bytes_accessed=2 ** 25, transcendentals=work),
        name="attn_bwd")(index, query, d_att, kv_all, lse, delta, cos_t, sin_t)


def rotate(vec, cosine, sine):
    first = vec[..., :HALF]
    second = vec[..., HALF:]
    return jnp.concatenate([first * cosine - second * sine, second * cosine + first * sine], axis=-1)


def matmul(left, right):
    return jnp.dot(left, right, preferred_element_type=jnp.float32)


def matmul_tn(left, right):
    return lax.dot_general(left, right, (((0,), (0,)), ((), ())), preferred_element_type=jnp.float32)


def matmul_nt(left, right):
    return lax.dot_general(left, right, NT_DIMS, preferred_element_type=jnp.float32)


def solution(mesh):
    def device_step(hidden, d_out, positions, norm_gain, w_query, b_query, w_key, b_key, w_value, b_value, w_out):
        batch, tokens, d_model = hidden.shape
        rows = batch * tokens
        kv_heads = w_key.shape[1] // HEAD_DIM
        group_width = d_model // kv_heads
        index = lax.axis_index('sp').astype(jnp.int32).reshape(1)
        f32 = jnp.float32
        bf16 = jnp.bfloat16

        inv_freq = ROPE_BASE ** (-jnp.arange(HALF, dtype=f32) * (2.0 / HEAD_DIM))
        angles = positions.astype(f32)[..., None] * inv_freq
        cosine = jnp.cos(angles).reshape(rows, 1, HALF)
        sine = jnp.sin(angles).reshape(rows, 1, HALF)
        cos_t = jnp.swapaxes(cosine.reshape(batch, tokens, HALF), 1, 2)
        sin_t = jnp.swapaxes(sine.reshape(batch, tokens, HALF), 1, 2)

        x_rows = hidden.reshape(rows, d_model)
        dy_rows = d_out.reshape(rows, d_model)
        x_f = x_rows.astype(f32)
        inv_rms = lax.rsqrt(jnp.mean(x_f * x_f, axis=-1, keepdims=True) + NORM_EPS)
        gain = norm_gain.astype(f32)
        normed = (x_f * inv_rms * gain).astype(bf16)

        k_pre = (matmul(normed, w_key) + b_key.astype(f32)).reshape(rows, kv_heads, HEAD_DIM)
        keys = rotate(k_pre, cosine, sine).astype(bf16)
        values = (matmul(normed, w_value) + b_value.astype(f32)).astype(bf16).reshape(rows, kv_heads, HEAD_DIM)
        kv_all = []
        for g in range(kv_heads):
            kv = jnp.concatenate([keys[:, g], values[:, g]], axis=-1).reshape(batch, tokens, 2 * HEAD_DIM)
            kv_all.append(lax.all_gather(kv, 'sp', axis=0))

        q_pre = (matmul(normed, w_query) + b_query.astype(f32)).reshape(rows, d_model // HEAD_DIM, HEAD_DIM)
        query = rotate(q_pre, cosine, sine).astype(bf16).reshape(rows, d_model)
        d_att = matmul_nt(dy_rows, w_out).astype(bf16)

        fwd = [attn_forward(index, query, d_att, kv_all[g], g, kv_heads) for g in range(kv_heads)]
        attended = jnp.concatenate([f[0] for f in fwd], axis=1)
        block_out = (x_f + matmul(attended, w_out)).astype(bf16)
        d_w_out = lax.psum(matmul_tn(attended, dy_rows), 'sp')

        d_query, d_b_query, d_w_query, d_keys, d_values = [], [], [], [], []
        for g in range(kv_heads):
            _, lse, delta = fwd[g]
            dq, dbq, dkv = attn_backward(index, query, d_att, kv_all[g], lse, delta, cos_t, sin_t, g, kv_heads)
            dkv = lax.psum_scatter(dkv, 'sp', scatter_dimension=0).reshape(rows, 2 * HEAD_DIM)
            d_query.append(dq)
            d_b_query.append(dbq)
            d_w_query.append(lax.psum(matmul_tn(normed, dq), 'sp'))
            d_keys.append(rotate(dkv[:, :HEAD_DIM], cosine[:, 0], -sine[:, 0]))
            d_values.append(dkv[:, HEAD_DIM:])

        dk_pre = jnp.concatenate(d_keys, axis=1)
        dv_pre = jnp.concatenate(d_values, axis=1)
        dk_bf = dk_pre.astype(bf16)
        dv_bf = dv_pre.astype(bf16)
        dq_bf = jnp.concatenate(d_query, axis=1)
        d_w_key, d_w_value = lax.psum((matmul_tn(normed, dk_bf), matmul_tn(normed, dv_bf)), 'sp')
        d_normed = matmul_nt(dq_bf, w_query) + matmul_nt(dk_bf, w_key) + matmul_nt(dv_bf, w_value)
        unit = x_f * inv_rms
        d_unit = d_normed * gain
        d_input = inv_rms * (d_unit - unit * jnp.mean(d_unit * unit, axis=-1, keepdims=True))
        d_hidden = (dy_rows.astype(f32) + d_input).astype(bf16)
        d_gain, d_bq, d_bk, d_bv = lax.psum((jnp.sum(d_normed * unit, axis=0), jnp.concatenate(d_b_query, axis=1)[0],
                                             jnp.sum(dk_pre, axis=0), jnp.sum(dv_pre, axis=0)), 'sp')
        return (block_out.reshape(hidden.shape), d_hidden.reshape(hidden.shape), d_gain,
                jnp.concatenate(d_w_query, axis=1), d_bq, d_w_key, d_bk, d_w_value, d_bv, d_w_out)

    seq_spec = P('dp', 'sp', None)
    in_specs = (seq_spec, seq_spec, P('dp', 'sp'), P(), P(), P(), P(), P(), P(), P(), P())
    out_specs = (seq_spec, seq_spec, P('dp'), P('dp', None), P('dp'), P('dp', None), P('dp'),
                 P('dp', None), P('dp'), P('dp', None))
    return jax.shard_map(device_step, mesh=mesh, in_specs=in_specs, out_specs=out_specs, check_vma=False)
```

time: 2260 us -> 1220 us (0.54)
  matrix products: 965 us -> 193 us
  local copies, waits for them, and re-layouts: 268 us -> 99.4 us
  other arithmetic: 241 us -> 75.1 us
  Pallas kernels: 0 us -> 96.1 us
  starting transfers between devices: 30.8 us -> 0.42 us
    dot_general x40 -> x13, matrix products: 965 us -> 193 us  [the longest x4 73.1 us: matmul_nt(): lax.dot_general(left, right, NT_DIMS, preferred_element_type=jnp.float32)]
    all_to_all x8 -> x0, waiting for transfers between devices: 391 us -> none  [the longest x1 84.7 us: device_step(): d_keys = lax.all_to_all(dk_h.astype(wire_type), 'sp', 1, 2, tiled=True)]
    reduce_scatter x0 -> x2, waiting for transfers between devices: none -> 384 us  [device_step(): lax.psum_scatter(dkv, 'sp', scatter_dimension=0).reshape(rows, 2 * HEAD_DIM)]
    reduce_sum x11 -> x3, other arithmetic: 123 us -> 5.55 us  [the longest x1 5.08 us: device_step(): inv_rms = lax.rsqrt(jnp.mean(x_f * x_f, axis=-1, keepdims=True) + NORM_EPS)]
    pallas_call x0 -> x4, Pallas kernels: none -> 96.1 us  [the longest x2 48.2 us: attn_backward(): pl.pallas_call(attn_bwd_kernel, grid_spec=grid_spec, out_shape=[jax.Shape...]
    all_to_all x8 -> x0, local copies, waits for them, and re-layouts: 70.2 us -> none  [the longest x2 25.4 us: device_step(): lax.all_to_all(attended_h.reshape(batch, seq, heads_local, HEAD_DIM), 'sp...]
    another operation x4 -> x0, local copies, waits for them, and re-layouts: 43.5 us -> none  [the longest x1 16.4 us: device_step(): dq_h.reshape(batch, seq, heads_local, HEAD_DIM)]
    reshape x4 -> x0, local copies, waits for them, and re-layouts: 35.1 us -> none  [the longest x1 14.5 us: device_step(): attended = attended.reshape(batch, tokens, d_model)]
  transfers between devices with their start and end apart: 9 -> 5, of which waited for: 8 -> 3; matrix products, arithmetic and copies ran while one was open for 17% -> 22% of each run, Pallas kernels for 0% -> 8%
where the time goes in v1:
time: 1220 us; the launch traced here: 1210 us
  waiting for transfers between devices  705 us (58%)
  matrix products  193 us (16%)
  local copies, waits for them, and re-layouts  99.4 us (8%)
  Pallas kernels  96.1 us (8%)
  other arithmetic  75.1 us (6%)
  blocking collectives  23.3 us (2%)
  between operations  14.7 us (1%)
    reduce_scatter x2, waiting for transfers between devices, device_step(): lax.psum_scatter(dkv, 'sp', scatter_dimension=0).reshape(rows, 2 * HEAD_DIM)  384 us
    psum x1, waiting for transfers between devices, device_step(): d_w_query.append(lax.psum(matmul_tn(normed, dq), 'sp'))  321 us
    dot_general x4, matrix products, matmul_nt(): lax.dot_general(left, right, NT_DIMS, preferred_element_type=jnp.float32)  73.1 us
    unnamed x99, local copies, waits for them, and re-layouts  72.8 us
    dot_general x4, matrix products, matmul(): return jnp.dot(left, right, preferred_element_type=jnp.float32)  60.8 us
    dot_general x5, matrix products, matmul_tn(): lax.dot_general(left, right, (((0,), (0,)), ((), ())), preferred_element_...  59.3 us
    pallas_call x2, Pallas kernels, attn_backward(): pl.pallas_call(attn_bwd_kernel, grid_spec=grid_spec, out_shape=[jax.Shape...  48.2 us
    pallas_call x2, Pallas kernels, attn_forward(): pl.pallas_call(attn_fwd_kernel, grid_spec=grid_spec, out_shape=[jax.Shape...  48 us
  transfers between devices with their start and end apart: 5, of which 3 were waited for; matrix products, arithmetic and copies ran while one was open for 22% of the time, Pallas kernels for 8%

profile of v1, /device:TPU:0, one launch (start us, length us, event | category | flops | bytes accessed | tf_op | source)
XLA Modules:
  0.0 1207.2 jit_solution(14597640998433543959)
XLA Ops:
  8.1 5.1 fusion.11
  13.2 8.8 fusion.4
  22.0 5.8 fusion.16
  28.9 1.9 multiply_cosine_fusion.1
  30.8 6.0 convolution_add_fusion.2
  38.0 2.0 copy.39
  40.1 2.3 pad_maximum_fusion.4
  43.9 2.1 pad_maximum_fusion.5
  47.8 24.5 %convolution_add_fusion = f32[2048,2048]{0,1:T(8,128)} fusion(bf16[2048,2048]{1,0:T(8,128)(2,1)} %fusion.4, bf16[2048,2048]{1,0:T(8,128)(2,1)} %param.15, f32[2048]{0:T(1024)S(1)} %convert_element_type.59), kind=kOutput, calls=%fused_computation.20 | convolution fusion | flops 17184063488 | bytes 33562624 | tf_op jit(solution)/shard_map/dot_general | solution.py:195
  72.4 10.8 fusion.41
  83.1 14.5 %copy.48 = f32[2048,16,64]{2,1,0:T(8,128)} copy(f32[2048,16,64]{0,2,1:T(8,128)} %get-tuple-element.47) | data formatting | bytes 16777216
  97.6 14.6 %copy.47 = f32[2048,16,64]{2,1,0:T(8,128)} copy(f32[2048,16,64]{0,2,1:T(8,128)} %get-tuple-element.48) | data formatting | bytes 16777216
  112.3 12.0 subtract_convert_fusion
  124.2 6.1 pad_maximum_fusion.1
  130.3 3.2 multiply_sine_fusion
  133.6 10.9 copy.57
  144.5 23.6 %convolution_convert_fusion.do_ref = bf16[2048,2048]{1,0:T(8,128)(2,1)} fusion(bf16[2048,2048]{1,0:T(8,128)(2,1)} %bitcast.83, bf16[2048,2048]{1,0:T(8,128)(2,1)} %param.21), kind=kOutput, calls=%fused_computation.26 | convolution fusion | flops 17184063488 | bytes 25165824 | tf_op jit(solution)/shard_map/dot_general | solution.py:203
  168.1 24.0 %attn_fwd.2 = (bf16[2048,1024]{1,0:T(8,128)(2,1)}, f32[8,8,256]{2,1,0:T(8,128)}, f32[8,8,256]{2,1,0:T(8,128)}) custom-call(s32[1]{0:T(128)} %bitcast.1.index_ref, bf16[2048,2048]{1,0:T(8,128)(2,1)} %bitcast.79, bf16[2048,2048]{1,0:T(8,128)(2,1)} %convolution_convert_fusion.do_ref, bf16[8,8,256,256]{3,2,1,0:T(8,128)(2,1)} %all-gather.3.cloned.1.call-done.kv_ref), custom_call_target="tpu_custom_call" | custom-call | flops 34359738368 | bytes 16777216 | tf_op jit(solution)/shard_map/attn_fwd/pallas_call | solution.py:157
  192.1 24.1 %attn_bwd.2 = (bf16[2048,1024]{1,0:T(8,128)(2,1)}, f32[1,1024]{1,0:T(1,128)}, f32[8,8,256,256]{3,2,1,0:T(8,128)}) custom-call(s32[1]{0:T(128)} %bitcast.1.index_ref, bf16[2048,2048]{1,0:T(8,128)(2,1)} %bitcast.80, bf16[2048,2048]{1,0:T(8,128)(2,1)} %convolution_convert_fusion.do_ref, bf16[8,8,256,256]{3,2,1,0:T(8,128)(2,1)} %all-gather.3.cloned.1.call-done.kv_ref, ...), custom_call_target="tpu_custom_call" | custom-call | flops 85899345920 | bytes 33554432 | tf_op jit(solution)/shard_map/attn_bwd/pallas_call | solution.py:178
  216.3 24.0 %attn_fwd.3 = (bf16[2048,1024]{1,0:T(8,128)(2,1)}, f32[8,8,256]{2,1,0:T(8,128)}, f32[8,8,256]{2,1,0:T(8,128)}) custom-call(s32[1]{0:T(128)} %bitcast.1.index_ref, bf16[2048,2048]{1,0:T(8,128)(2,1)} %bitcast.81, bf16[2048,2048]{1,0:T(8,128)(2,1)} %convolution_convert_fusion.do_ref, bf16[8,8,256,256]{3,2,1,0:T(8,128)(2,1)} %all-gather.5.cloned.1.call-done.kv_ref), custom_call_target="tpu_custom_call" | custom-call | flops 34359738368 | bytes 16777216 | tf_op jit(solution)/shard_map/attn_fwd/pallas_call | solution.py:157
  240.3 24.1 %attn_bwd.3 = (bf16[2048,1024]{1,0:T(8,128)(2,1)}, f32[1,1024]{1,0:T(1,128)}, f32[8,8,256,256]{3,2,1,0:T(8,128)}) custom-call(s32[1]{0:T(128)} %bitcast.1.index_ref, bf16[2048,2048]{1,0:T(8,128)(2,1)} %bitcast.82, bf16[2048,2048]{1,0:T(8,128)(2,1)} %convolution_convert_fusion.do_ref, bf16[8,8,256,256]{3,2,1,0:T(8,128)(2,1)} %all-gather.5.cloned.1.call-done.kv_ref, ...), custom_call_target="tpu_custom_call" | custom-call | flops 85899345920 | bytes 33554432 | tf_op jit(solution)/shard_map/attn_bwd/pallas_call | solution.py:178
  264.5 2.8 constant_dynamic-update-slice_fusion.1
  269.2 3.2 copy-done.34
  272.4 2.4 slice-done.5
  274.8 11.9 fusion.47
  286.7 11.5 fusion.46
  298.2 21.3 %fusion.48 = f32[2048,2048]{1,0:T(8,128)} fusion(bf16[2048,2048]{1,0:T(8,128)(2,1)S(1)} %constant_dynamic-update-slice_fusion, bf16[2048,2048]{1,0:T(8,128)(2,1)S(1)} %bitcast.86), kind=kOutput, calls=%fused_computation.77 | convolution fusion | flops 17179869184 | bytes 33554432 | tf_op jit(solution)/shard_map/dot_general | solution.py:199
  319.5 173.3 %reduce-scatter.3.cloned.1.call-done = f32[1,8,256,256]{3,2,1,0:T(8,128)} async-done(((f32[8,8,256,256]{3,2,1,0:T(8,128)}), f32[1,8,256,256]{3,2,1,0:T(8,128)}) %reduce-scatter.3.cloned.1.call-update) | async-done | bytes 2097168 | tf_op jit(solution)/shard_map/reduce_scatter | solution.py:251
  494.1 3.2 fusion.42
  497.4 210.9 %reduce-scatter.5.cloned.1.call-done = f32[1,8,256,256]{3,2,1,0:T(8,128)} async-done(((f32[8,8,256,256]{3,2,1,0:T(8,128)}), f32[1,8,256,256]{3,2,1,0:T(8,128)}) %reduce-scatter.5.cloned.1.call-update) | async-done | bytes 2097168 | tf_op jit(solution)/shard_map/reduce_scatter | solution.py:251
  709.5 3.2 fusion.43
  712.7 2.3 copy.49
  715.1 2.3 copy.50
  717.4 2.3 copy.51
  719.8 2.3 copy.52
  722.1 7.3 fusion.30
  729.5 2.4 fusion.25
  733.2 7.2 fusion.37
  741.3 24.5 %fusion.12 = bf16[2048,2048]{1,0:T(8,128)(2,1)} fusion(bf16[8,256,2048]{2,1,0:T(8,128)(2,1)} %param.11, bf16[2048,2048]{1,0:T(8,128)(2,1)} %copy-done.15, bf16[2048,2048]{1,0:T(8,128)(2,1)} %param.21), kind=kOutput, calls=%fused_computation.16 | convolution fusion | flops 17192452096 | bytes 33554432 | tf_op jit(solution)/shard_map/dot_general | solution.py:195
  766.3 8.5 fusion.32
  774.8 8.6 fusion.39
  783.4 32.4 %fusion.10 = (f32[2048]{0:T(1024)S(1)}, f32[2048]{0:T(1024)S(1)}, f32[2048,2048]{1,0:T(8,128)}) fusion(bf16[8,256,2048]{2,1,0:T(8,128)(2,1)} %param.11, f32[2048]{0:T(1024)S(1)} %bitcast.101, f32[2048]{0:T(1024)S(1)} %copy-done.22, f32[2048,2048]{1,0:T(8,128)} %fusion.32, f32[2048,2048]{1,0:T(8,128)} %fusion.39, bf16[2048,2048]{1,0:T(8,128)(2,1)} %param.15, ...), kind=kOutput, calls=%fused_computation.14 | convolution fusion | flops 17234391040 | bytes 75530240 | tf_op jit(solution)/shard_map/dot_general | solution.py:203
  815.8 23.3 %all-reduce = (f32[2048]{0:T(1024)}, f32[2048]{0:T(1024)}, f32[256]{0:T(256)}, f32[256]{0:T(256)}) all-reduce(f32[2048]{0:T(1024)S(1)} %get-tuple-element.34, f32[2048]{0:T(1024)S(1)} %bitcast.103, f32[256]{0:T(256)S(1)} %fusion.19, f32[256]{0:T(256)S(1)} %fusion.17), channel_id=1, replica_groups=mesh['dp'=1,'sp'=8] {'sp'}, use_global_device_ids=true, to_apply=%region_5.0 | all-reduce | flops 4608 | bytes 36864 | tf_op jit(solution)/shard_map/psum | solution.py:269
  839.1 14.9 %fusion.9 = bf16[2048,2048]{1,0:T(8,128)(2,1)} fusion(bf16[8,256,2048]{2,1,0:T(8,128)(2,1)} %param.11, f32[2048,2048]{1,0:T(8,128)} %get-tuple-element.71, f32[2048]{0:T(1024)S(1)} %broadcast_multiply_fusion, f32[2048]{0:T(1024)S(1)} %copy-done.22, f32[2048]{0:T(1024)S(1)} %bitcast.102, bf16[8,256,2048]{2,1,0:T(8,128)(2,1)} %param.12), kind=kLoop, calls=%fused_computation.13 | loop fusion | flops 37748736 | bytes 41967616 | tf_op jit(solution)/shard_map/convert_element_type | solution.py:268
  854.0 320.8 %all-reduce.4.cloned.1.call-done = (f32[2048,1024]{1,0:T(8,128)}, f32[2048,1024]{1,0:T(8,128)}, f32[2048,256]{1,0:T(8,128)}, f32[2048,256]{1,0:T(8,128)}, f32[2048,2048]{1,0:T(8,128)}) async-done(((f32[2048,1024]{1,0:T(8,128)}, f32[2048,1024]{1,0:T(8,128)}, f32[2048,256]{1,0:T(8,128)}, f32[2048,256]{1,0:T(8,128)}, f32[2048,2048]{1,0:T(8,128)}), (f32[2048,1024]{1,0:T(8,128)}, f32[2048,1024]{1,0:T(8,128)}, ...) | async-done | bytes 37748752 | tf_op jit(solution)/shard_map/psum | solution.py:254
  1174.8 13.8 %pad_maximum_fusion = f32[2048,2048]{1,0:T(8,128)} fusion(f32[2048,1024]{1,0:T(8,128)} %get-tuple-element.40, f32[2048,1024]{1,0:T(8,128)} %get-tuple-element.41), kind=kLoop, calls=%fused_computation | loop fusion | flops 4194304 | bytes 33554432 | tf_op jit(solution)/shard_map/concatenate | solution.py:272
  1191.3 1.7 slice-done.2
  1194.1 6.2 copy.66
  (124 shorter events, 17.4 us)
Async XLA Ops:
  7.2 14.9 %copy-start = (bf16[2048,256]{1,0:T(8,128)(2,1)S(1)}, bf16[2048,256]{1,0:T(8,128)(2,1)}, u32[]{:S(2)}) copy-start(bf16[2048,256]{1,0:T(8,128)(2,1)} %param.19) | copy-start | bytes 3145732
  7.2 6.0 copy-start.25
  7.2 6.0 copy-start.31
  7.2 160.9 %all-gather.3.cloned.1.call-start = ((), (), s32[]{:S(2)}) async-start(), calls=%async_computation.2 | async-start | bytes 9437184 | tf_op jit(solution)/shard_map/all_gather | solution.py:236
  7.3 123.1 %copy-start.26 = (f32[64]{0:T(128)}, f32[64]{0:T(128)S(1)}, u32[]{:S(2)}) copy-start(f32[64]{0:T(128)S(1)} %multiply_power_fusion) | copy-start | bytes 772
  8.0 14.0 %copy-start.21 = (f32[2048]{0:T(1024)}, f32[2048]{0:T(1024)S(1)}, u32[]{:S(2)}) copy-start(f32[2048]{0:T(1024)S(1)} %convert_element_type.57) | copy-start | bytes 24580
  13.2 8.9 copy-start.23
  13.2 15.7 %copy-start.19 = (f32[1,2,8,128]{3,1,2,0:T(2,128)}, f32[1,2,8,128]{3,1,2,0:T(2,128)S(1)}, u32[]{:S(2)}) copy-start(f32[1,2,8,128]{3,1,2,0:T(2,128)S(1)} %copy.54) | copy-start | bytes 24580
  22.0 6.9 copy-start.32
  37.2 10.7 copy-start.28
  42.4 173.9 %all-gather.5.cloned.1.call-start = ((), (), s32[]{:S(2)}) async-start(), calls=%async_computation.3 | async-start | bytes 9437184 | tf_op jit(solution)/shard_map/all_gather | solution.py:236
  46.1 446.7 %reduce-scatter.3.cloned.1.call-start = ((), (), s32[]{:S(2)}) async-start(), calls=%async_computation.4 | async-start | bytes 18874368 | tf_op jit(solution)/shard_map/reduce_scatter | solution.py:251
  97.6 14.6 %copy-start.9 = (f32[2048,64]{1,0:T(8,128)S(1)}, f32[2048,64]{1,0:T(8,128)}, u32[]{:S(2)}) copy-start(f32[2048,64]{1,0:T(8,128)} %copy.36) | copy-start | bytes 1572868
  216.2 492.0 %reduce-scatter.5.cloned.1.call-start = ((), (), s32[]{:S(2)}) async-start(), calls=%async_computation.5 | async-start | bytes 18874368 | tf_op jit(solution)/shard_map/reduce_scatter | solution.py:251
  264.4 910.4 %all-reduce.4.cloned.1.call-start = ((), (), s32[]{:S(2)}) async-start(), calls=%async_computation.6 | async-start | bytes 75497472 | tf_op jit(solution)/shard_map/psum | solution.py:254
  264.5 3.5 copy-start.10
  264.5 4.7 slice-start.4
  264.5 7.9 copy-start.34
  267.9 6.9 slice-start.5
  268.6 29.7 %copy-start.15 = (bf16[2048,2048]{1,0:T(8,128)(2,1)}, bf16[2048,2048]{1,0:T(8,128)(2,1)S(1)}, u32[]{:S(2)}) copy-start(bf16[2048,2048]{1,0:T(8,128)(2,1)S(1)} %constant_dynamic-update-slice_fusion) | copy-start | bytes 25165828
  274.8 11.9 copy-start.33
  274.8 23.4 %slice-start.6 = ((s8[8388608]{0:T(1024)(128)(4,1)}), s8[4194304]{0:T(1024)(128)(4,1)S(1)}, s32[]{:S(2)}) async-start(s8[8388608]{0:T(1024)(128)(4,1)} %bitcast.84), calls=%async_computation.13 | async-start | bytes 8388608
  286.7 11.5 slice-start.7
  722.1 7.4 copy-start.11
  722.1 7.4 copy-start.12
  722.1 7.4 copy-start.13
  722.1 7.4 copy-start.14
  722.1 7.4 copy-start.20
  722.1 7.4 copy-start.27
  731.9 0.8 copy-start.1
  731.9 1.0 copy-start.3
  731.9 1.1 copy-start.5
  732.0 1.3 copy-start.7
  740.5 0.7 copy-start.29
  740.5 0.7 copy-start.30
  741.2 24.9 %copy-start.2 = (f32[2048,64]{0,1:T(8,128)S(1)}, f32[2048,64]{0,1:T(8,128)}, u32[]{:S(2)}) copy-start(f32[2048,64]{0,1:T(8,128)} %copy-done.1) | copy-start | bytes 1572868
  741.2 24.9 %copy-start.4 = (f32[2048,64]{0,1:T(8,128)S(1)}, f32[2048,64]{0,1:T(8,128)}, u32[]{:S(2)}) copy-start(f32[2048,64]{0,1:T(8,128)} %copy-done.3) | copy-start | bytes 1572868
  741.2 24.9 %copy-start.6 = (f32[2048,64]{0,1:T(8,128)S(1)}, f32[2048,64]{0,1:T(8,128)}, u32[]{:S(2)}) copy-start(f32[2048,64]{0,1:T(8,128)} %copy-done.5) | copy-start | bytes 1572868
  741.2 24.9 %copy-start.8 = (f32[2048,64]{0,1:T(8,128)S(1)}, f32[2048,64]{0,1:T(8,128)}, u32[]{:S(2)}) copy-start(f32[2048,64]{0,1:T(8,128)} %copy-done.7) | copy-start | bytes 1572868
  766.3 8.5 copy-start.18
  774.8 8.6 copy-start.22
  774.8 8.6 copy-start.24
  1174.8 16.4 %slice-start = ((s8[16777216]{0:T(1024)(128)(4,1)}), s8[4194304]{0:T(1024)(128)(4,1)S(1)}, s32[]{:S(2)}) async-start(s8[16777216]{0:T(1024)(128)(4,1)} %bitcast.74), calls=%async_computation.7 | async-start | bytes 8388608
  1174.8 13.8 %copy-start.17 = (f32[2048,256]{1,0:T(8,128)S(1)}, f32[2048,256]{1,0:T(8,128)}, u32[]{:S(2)}) copy-start(f32[2048,256]{1,0:T(8,128)} %get-tuple-element.77) | copy-start | bytes 6291460
  1174.8 15.1 %copy-start.16 = (f32[2048,256]{1,0:T(8,128)S(1)}, f32[2048,256]{1,0:T(8,128)}, u32[]{:S(2)}) copy-start(f32[2048,256]{1,0:T(8,128)} %get-tuple-element.79) | copy-start | bytes 6291460
  1174.8 16.4 %slice-start.1 = ((s8[16777216]{0:T(1024)(128)(4,1)}), s8[4194304]{0:T(1024)(128)(4,1)S(1)}, s32[]{:S(2)}) async-start(s8[16777216]{0:T(1024)(128)(4,1)} %bitcast.74), calls=%async_computation.8 | async-start | bytes 8388608
  1174.8 18.1 %slice-start.2 = ((s8[16777216]{0:T(1024)(128)(4,1)}), s8[4194304]{0:T(1024)(128)(4,1)S(1)}, s32[]{:S(2)}) async-start(s8[16777216]{0:T(1024)(128)(4,1)} %bitcast.74), calls=%async_computation.9 | async-start | bytes 8388608
  1174.8 19.3 %slice-start.3 = ((s8[16777216]{0:T(1024)(128)(4,1)}), s8[4194304]{0:T(1024)(128)(4,1)S(1)}, s32[]{:S(2)}) async-start(s8[16777216]{0:T(1024)(128)(4,1)} %bitcast.74), calls=%async_computation.10 | async-start | bytes 8388608
Sparse Core Ops, SparseCore 0:
  42.5 51.1 all-gather.2
  95.5 48.3 all-gather.4
  216.4 276.4 reduce-scatter.2
  496.7 211.4 reduce-scatter.4
  740.6 434.1 all-reduce.3
